TPU v7x, 8 devices: a whole 2x2x1 slice. The times are simulated.
8 devices in a mesh: dp: 1 (over z), ri: 2 (over y), co: 2 (over x), ro: 2 (over core).
Axes of the slice: x: 2, y: 2, z: 1, core: 2. Of those that a mesh axis runs over, the one named last changes fastest.
Arguments:
- a_mat: bfloat16 [4096, 32768], P(('dp', 'ri', 'ro'), 'co')
- b_mat: bfloat16 [32768, 16384], P(('dp', 'ri', 'ro'), 'co')
Outputs:
- output: bfloat16 [4096, 16384], P(('dp', 'ri', 'ro'), 'co')
All inputs are finite; a program needn't handle non-finite values.
Results may differ from a plain program's by a relative error of at most 0.001.
Values are sent between devices in bfloat16 or wider.
A program may use at most 1 GiB of HBM per device.

v0:
```python
import jax
import jax.numpy as jnp
from jax import lax
from jax.sharding import PartitionSpec as P, NamedSharding


def solution(mesh):
    grid_spec = P(("dp", "ri", "ro"), "co")

    def local_block(a_block, b_block):
        a_rows = lax.all_gather(a_block, "co", axis=1, tiled=True)
        b_cols = lax.all_gather(b_block, ("ri", "ro"), axis=0, tiled=True)
        product = jnp.dot(a_rows, b_cols, preferred_element_type=jnp.float32)
        return product.astype(jnp.bfloat16)

    return jax.shard_map(local_block, mesh=mesh, in_specs=(grid_spec, grid_spec), out_specs=grid_spec, check_vma=False)
```

profile of v0, /device:TPU:2, one launch (start us, length us, event | category | flops | bytes accessed | tf_op | source)
XLA Modules:
  0.0 4417.2 jit_solution(6882496162253001739)
XLA Ops:
  6.5 0.0 all-gather.3.cloned.1.call-start
  6.5 0.7 all-gather.3.cloned.1.call-update
  7.3 0.0 all-gather.5.cloned.1.call-start
  7.3 0.7 all-gather.5.cloned.1.call-update
  8.0 763.9 %all-gather.3.cloned.1.call-done = bf16[1024,32768]{1,0:T(8,128)(2,1)} async-done(((bf16[1024,16384]{1,0:T(8,128)(2,1)}), bf16[1024,32768]{1,0:T(8,128)(2,1)}) %all-gather.3.cloned.1.call-update) | async-done | bytes 67108880 | tf_op jit(solution)/shard_map/all_gather | solution.py:11
  771.9 3056.9 %all-gather.5.cloned.1.call-done = bf16[32768,8192]{1,0:T(8,128)(2,1)} async-done(((bf16[8192,8192]{1,0:T(8,128)(2,1)}), bf16[32768,8192]{1,0:T(8,128)(2,1)}) %all-gather.5.cloned.1.call-update) | async-done | bytes 536870912 | tf_op jit(solution)/shard_map/all_gather | solution.py:12
  3828.7 581.6 %convolution_convert_fusion = bf16[1024,8192]{1,0:T(8,128)(2,1)} fusion(bf16[1024,32768]{1,0:T(8,128)(2,1)} %all-gather.3.cloned.1.call-done, bf16[32768,8192]{1,0:T(8,128)(2,1)} %all-gather.5.cloned.1.call-done), kind=kOutput, calls=%fused_computation | convolution fusion | flops 549764202496 | bytes 620756992 | tf_op jit(solution)/shard_map/dot_general | solution.py:13
Async XLA Ops:
  6.5 765.3 %all-gather.3.cloned.1.call-start = ((), (), s32[]{:S(2)}) async-start(), calls=%async_computation | async-start | bytes 100663296 | tf_op jit(solution)/shard_map/all_gather | solution.py:11
  7.3 3821.5 %all-gather.5.cloned.1.call-start = ((), (), s32[]{:S(2)}) async-start(), calls=%async_computation.1 | async-start | bytes 671088640 | tf_op jit(solution)/shard_map/all_gather | solution.py:12
Sparse Core Ops, SparseCore 0:
  8.8 762.9 all-gather.2
  773.4 3055.2 all-gather.4
where the time goes:
time: 4420 us
  waiting for transfers between devices  3820 us (86%)
  matrix products  582 us (13%)
    all_gather x1, waiting for transfers between devices, local_block(): b_cols = lax.all_gather(b_block, ('ri', 'ro'), axis=0, tiled=True)  3060 us
    all_gather x1, waiting for transfers between devices, local_block(): a_rows = lax.all_gather(a_block, 'co', axis=1, tiled=True)  764 us
    dot_general x1, matrix products, local_block(): product = jnp.dot(a_rows, b_cols, preferred_element_type=jnp.float32)  582 us
  transfers between devices with their start and end apart: 2, of which 2 were waited for; matrix products, arithmetic and copies ran while one was open for 0% of the time, Pallas kernels for 0%

commit v1 on v0

v1 whole, which is shorter than its diff:
```python
import functools

import jax
import jax.numpy as jnp
from jax import lax
from jax.experimental import pallas as pl
from jax.experimental.pallas import tpu as pltpu
from jax.sharding import PartitionSpec as P

MESH = pl.DeviceIdType.MESH
UNITS = 4
B_BUFFERS = 3


def make_sizes(rows, k_half, cols):
    k_quarter = k_half // 2
    return dict(
        rows=rows,
        k_half=k_half,
        k_quarter=k_quarter,
        cols=cols,
        unit=rows // UNITS,
        tile=cols // 8,
        x0_depth=k_quarter // 8,
        x1_depth=k_quarter // 4,
    )


def kernel(sizes, a, b, out, b_far, x0, x1, stage, part, acc, far_s, far_r, x0_s, x0_r, x1_s, x1_r, fwd_s, part_s, part_r, b_sem, x_sem, o_sem):
    rows, k_half, k_quarter = sizes["rows"], sizes["k_half"], sizes["k_quarter"]
    unit, tile = sizes["unit"], sizes["tile"]
    n_tiles = sizes["cols"] // tile
    i, j, r = lax.axis_index("ri"), lax.axis_index("co"), lax.axis_index("ro")
    dp = lax.axis_index("dp")
    vertical, horizontal = (dp, 1 - i, j, r), (dp, i, 1 - j, r)
    opposite, partner = (dp, 1 - i, 1 - j, r), (dp, i, j, 1 - r)
    diag = i == j
    off = jnp.logical_not(diag)

    barrier = pltpu.get_barrier_semaphore()
    for device in (vertical, horizontal, opposite, partner):
        pl.semaphore_signal(barrier, inc=1, device_id=device, device_id_type=MESH)
    pl.semaphore_wait(barrier, 4)

    def remote(src, dst, send, recv, device):
        return pltpu.make_async_remote_copy(
            src_ref=src, dst_ref=dst, send_sem=send, recv_sem=recv, device_id=device, device_id_type=MESH
        )

    far_rows = k_quarter // 8

    def far_copy(c):
        block = pl.ds(c * far_rows, far_rows)
        return remote(b.at[block], b_far.at[block], far_s.at[c], far_r.at[c], partner)

    def k_column(kc, depth):
        return pl.multiple_of(lax.rem(r * k_quarter + kc * depth, k_half), depth)

    x0_depth = sizes["x0_depth"]
    n_x0 = k_half // x0_depth

    def x0_copy(kc):
        block = pl.ds(k_column(kc, x0_depth), x0_depth)
        return remote(a.at[:, block], x0.at[:, block], x0_s.at[kc], x0_r.at[kc], horizontal)

    def unit_rows(u):
        return pl.ds(pl.multiple_of(u * unit, unit), unit)

    def x1_send(u, device):
        return remote(a.at[unit_rows(u)], x1.at[unit_rows(u)], x1_s.at[u], x1_r.at[u], device)

    def x1_forward(u):
        return remote(x1.at[unit_rows(u)], x1.at[unit_rows(u)], fwd_s.at[u], x1_r.at[u], horizontal)

    def tile_cols(t):
        return pl.ds(pl.multiple_of(t * tile, tile), tile)

    def part_copy(u, t):
        where = (unit_rows(u), tile_cols(t))
        return remote(stage.at[where], part.at[where], part_s.at[u * n_tiles + t], part_r.at[u * n_tiles + t], vertical)

    def each(n, step):
        def body(c, carry):
            step(c)
            return carry

        lax.fori_loop(0, n, body, 0)

    def own_rows(first, last, source, b_source, ready=None, b_ready=None):
        base = first if first < n_x0 // 2 else first - n_x0 // 2
        steps = (last - first) * n_tiles

        def scope(xbuf, bbuf):
            def b_copy(s):
                c = lax.div(s, n_tiles)
                t = lax.rem(s, n_tiles)
                slot = lax.rem(s, B_BUFFERS)
                k_rows = pl.ds(pl.multiple_of((base + c) * x0_depth, x0_depth), x0_depth)
                return pltpu.make_async_copy(b_source.at[k_rows, tile_cols(t)], bbuf.at[slot], b_sem.at[slot])

            def b_start(s):
                if b_ready is not None:

                    @pl.when(lax.rem(s, n_tiles) == 0)
                    def _():
                        b_ready(base + lax.div(s, n_tiles))

                b_copy(s).start()

            for s in range(B_BUFFERS - 1):
                b_start(jnp.int32(s))

            def body(s, carry):
                c = lax.div(s, n_tiles)
                t = lax.rem(s, n_tiles)

                @pl.when(s + B_BUFFERS - 1 < steps)
                def _():
                    b_start(s + B_BUFFERS - 1)

                @pl.when(t == 0)
                def _():
                    if ready is not None:
                        ready(first + c)
                    block = pl.ds(k_column(first + c, x0_depth), x0_depth)
                    copy = pltpu.make_async_copy(source.at[:, block], xbuf, x_sem)
                    copy.start()
                    copy.wait()

                b_copy(s).wait()
                product = jnp.dot(xbuf[...], bbuf[lax.rem(s, B_BUFFERS)], preferred_element_type=jnp.float32)
                if first == 0:

                    @pl.when(c == 0)
                    def _():
                        acc[:, tile_cols(t)] = product

                    @pl.when(c > 0)
                    def _():
                        acc[:, tile_cols(t)] += product
                else:
                    acc[:, tile_cols(t)] += product
                return carry

            lax.fori_loop(0, steps, body, 0)

        pl.run_scoped(
            scope,
            pltpu.VMEM((rows, x0_depth), jnp.bfloat16),
            pltpu.VMEM((B_BUFFERS, x0_depth, tile), jnp.bfloat16),
        )

    x1_depth = sizes["x1_depth"]
    n_x1 = k_half // x1_depth

    def other_rows(u):
        steps = n_tiles * n_x1

        def scope(xbuf, bbuf, pbuf):
            def b_start(s):
                t = lax.div(s, n_x1)
                kc = lax.rem(s, n_x1)
                slot = lax.rem(s, B_BUFFERS)

                @pl.when(kc < n_x1 // 2)
                def _():
                    k_rows = pl.ds(pl.multiple_of(kc * x1_depth, x1_depth), x1_depth)
                    pltpu.make_async_copy(b.at[k_rows, tile_cols(t)], bbuf.at[slot], b_sem.at[slot]).start()

                @pl.when(kc >= n_x1 // 2)
                def _():
                    k_rows = pl.ds(pl.multiple_of((kc - n_x1 // 2) * x1_depth, x1_depth), x1_depth)
                    pltpu.make_async_copy(b_far.at[k_rows, tile_cols(t)], bbuf.at[slot], b_sem.at[slot]).start()

            load = pltpu.make_async_copy(x1.at[unit_rows(u)], xbuf, x_sem)
            load.start()
            for s in range(B_BUFFERS - 1):
                b_start(jnp.int32(s))
            load.wait()

            def body(s, carry):
                t = lax.div(s, n_x1)
                kc = lax.rem(s, n_x1)
                slot = lax.rem(s, B_BUFFERS)

                @pl.when(s + B_BUFFERS - 1 < steps)
                def _():
                    b_start(s + B_BUFFERS - 1)

                pltpu.make_async_copy(b.at[pl.ds(0, x1_depth), pl.ds(0, tile)], bbuf.at[slot], b_sem.at[slot]).wait()
                columns = pl.ds(k_column(kc, x1_depth), x1_depth)
                product = jnp.dot(xbuf[:, columns], bbuf[slot], preferred_element_type=jnp.float32)

                @pl.when(kc == 0)
                def _():
                    pbuf[...] = product

                @pl.when(kc > 0)
                def _():
                    pbuf[...] += product

                @pl.when(kc == n_x1 - 1)
                def _():
                    put = pltpu.make_async_copy(pbuf, stage.at[unit_rows(u), tile_cols(t)], o_sem)
                    put.start()
                    put.wait()
                    part_copy(u, t).start()

                return carry

            lax.fori_loop(0, steps, body, 0)

        pl.run_scoped(
            scope,
            pltpu.VMEM((unit, k_half), jnp.bfloat16),
            pltpu.VMEM((B_BUFFERS, x1_depth, tile), jnp.bfloat16),
            pltpu.VMEM((unit, tile), jnp.float32),
        )

    def finish(units):
        def scope(pbuf, obuf, p_sem, w_sem):
            steps = len(units) * n_tiles

            def place(s):
                u = jnp.int32(units[0])
                for q in range(1, len(units)):
                    u = jnp.where(lax.div(s, n_tiles) == q, jnp.int32(units[q]), u)
                return u, lax.rem(s, n_tiles)

            def start(s):
                u, t = place(s)
                slot = lax.rem(s, 2)
                part_copy(u, t).wait_recv()
                pltpu.make_async_copy(part.at[unit_rows(u), tile_cols(t)], pbuf.at[slot], p_sem.at[slot]).start()

            def put(s):
                u, t = place(s)
                slot = lax.rem(s, 2)
                return pltpu.make_async_copy(obuf.at[slot], out.at[unit_rows(u), tile_cols(t)], w_sem.at[slot])

            start(jnp.int32(0))

            def body(s, carry):
                u, t = place(s)
                slot = lax.rem(s, 2)

                @pl.when(s + 1 < steps)
                def _():
                    start(s + 1)

                @pl.when(s >= 2)
                def _():
                    put(s - 2).wait()

                pltpu.make_async_copy(part.at[unit_rows(u), tile_cols(t)], pbuf.at[slot], p_sem.at[slot]).wait()
                obuf[slot] = (acc[unit_rows(u), tile_cols(t)] + pbuf[slot]).astype(out.dtype)
                put(s).start()
                return carry

            lax.fori_loop(0, steps, body, 0)
            put(jnp.int32(steps - 2)).wait()
            put(jnp.int32(steps - 1)).wait()

        pl.run_scoped(
            scope,
            pltpu.VMEM((2, unit, tile), jnp.float32),
            pltpu.VMEM((2, unit, tile), out.dtype),
            pltpu.SemaphoreType.DMA((2,)),
            pltpu.SemaphoreType.DMA((2,)),
        )

    half = n_x0 // 2
    quarter = n_x0 // 4

    @pl.when(diag)
    def _():
        each(half, lambda c: x0_copy(c).start())
        each(8, lambda c: far_copy(c).start())
        own_rows(0, half, a, b)
        own_rows(half, n_x0, a, b_far, b_ready=lambda c: far_copy(c).wait_recv())
        for u in (0, 1):
            x1_forward(u).wait_recv()
            x1_forward(u).start()
            if u == 1:
                each(half, lambda c: x0_copy(c + half).start())
            other_rows(u)
        for u in (2, 3):
            x1_forward(u).wait_recv()
            other_rows(u)
        finish((2, 3, 0, 1))
        each(n_x0, lambda c: x0_copy(c).wait_send())
        for u in (0, 1):
            x1_forward(u).wait_send()

    @pl.when(off)
    def _():
        for u in (0, 1):
            x1_send(u, vertical).start()
        for u in (2, 3):
            x1_send(u, opposite).start()
        each(8, lambda c: far_copy(c).start())
        arrived = lambda c: x0_copy(c).wait_recv()
        own_rows(0, quarter, x0, b, ready=arrived)
        x1_forward(2).wait_recv()
        x1_forward(2).start()
        each(8, lambda c: far_copy(c).wait_recv())
        other_rows(2)
        own_rows(quarter, half, x0, b, ready=arrived)
        x1_forward(3).wait_recv()
        x1_forward(3).start()
        other_rows(3)
        for u in (0, 1):
            x1_forward(u).wait_recv()
            other_rows(u)
        own_rows(half, n_x0, x0, b_far, ready=arrived)
        finish((0, 1, 2, 3))
        for u in range(UNITS):
            x1_send(u, vertical).wait_send()
        for u in (2, 3):
            x1_forward(u).wait_send()

    each(8, lambda c: far_copy(c).wait_send())
    for u in range(UNITS):
        each(n_tiles, lambda t: part_copy(u, t).wait_send())


def solution(mesh):
    grid_spec = P(("dp", "ri", "ro"), "co")

    def local_block(a_block, b_block):
        rows, k_half = a_block.shape
        k_quarter, cols = b_block.shape
        sizes = make_sizes(rows, k_half, cols)
        n_x0 = k_half // sizes["x0_depth"]
        n_part = UNITS * (cols // sizes["tile"])
        dma = pltpu.SemaphoreType.DMA
        results = pl.pallas_call(
            functools.partial(kernel, sizes),
            out_shape=[
                jax.ShapeDtypeStruct((rows, cols), jnp.bfloat16),
                jax.ShapeDtypeStruct((k_quarter, cols), jnp.bfloat16),
                jax.ShapeDtypeStruct((rows, k_half), jnp.bfloat16),
                jax.ShapeDtypeStruct((rows, k_half), jnp.bfloat16),
                jax.ShapeDtypeStruct((rows, cols), jnp.float32),
                jax.ShapeDtypeStruct((rows, cols), jnp.float32),
            ],
            in_specs=[pl.BlockSpec(memory_space=pl.ANY)] * 2,
            out_specs=[pl.BlockSpec(memory_space=pl.ANY)] * 6,
            scratch_shapes=[
                pltpu.VMEM((rows, cols), jnp.float32),
                dma((8,)),
                dma((8,)),
                dma((n_x0,)),
                dma((n_x0,)),
                dma((UNITS,)),
                dma((UNITS,)),
                dma((UNITS,)),
                dma((n_part,)),
                dma((n_part,)),
                dma((B_BUFFERS,)),
                dma,
                dma,
            ],
            compiler_params=pltpu.CompilerParams(
                collective_id=0, has_side_effects=True, vmem_limit_bytes=63 * 1024 * 1024
            ),
        )(a_block, b_block)
        return results[0]

    return jax.shard_map(local_block, mesh=mesh, in_specs=(grid_spec, grid_spec), out_specs=grid_spec, check_vma=False)
```

time: 4420 us -> 1150 us (0.26)
  waiting for transfers between devices: 3820 us -> 0 us
  Pallas kernels: 0 us -> 1140 us
  matrix products: 582 us -> 0 us
    all_gather x2 -> x0, waiting for transfers between devices: 3820 us -> none  [the longest x1 3060 us: local_block(): b_cols = lax.all_gather(b_block, ('ri', 'ro'), axis=0, tiled=True)]
    pallas_call x0 -> x1, Pallas kernels: none -> 1140 us  [local_block(): pl.pallas_call(functools.partial(kernel, sizes), out_shape=[jax.ShapeDtyp...]
    dot_general x1 -> x0, matrix products: 582 us -> none  [local_block(): product = jnp.dot(a_rows, b_cols, preferred_element_type=jnp.float32)]
  transfers between devices with their start and end apart: 2 -> 0, of which waited for: 2 -> 0; matrix products, arithmetic and copies ran while one was open for 0% -> 0% of each run, Pallas kernels for 0% -> 0%
where the time goes in v1:
time: 1150 us
  Pallas kernels  1140 us (99%)
  local copies, waits for them, and re-layouts  14 us (1%)
    pallas_call x1, Pallas kernels, local_block(): pl.pallas_call(functools.partial(kernel, sizes), out_shape=[jax.ShapeDtyp...  1140 us

profile of v1, /device:TPU:2, one launch (start us, length us, event | category | flops | bytes accessed | tf_op | source)
XLA Modules:
  0.0 1152.0 jit_solution(3049193567403659552)
XLA Ops:
  0.0 1138.0 %shard_map.28 = (bf16[1024,8192]{1,0:T(8,128)(2,1)}, bf16[8192,8192]{1,0:T(8,128)(2,1)}, bf16[1024,16384]{1,0:T(8,128)(2,1)}, bf16[1024,16384]{1,0:T(8,128)(2,1)...) custom-call(bf16[1024,16384]{1,0:T(8,128)(2,1)} %a.1, bf16[8192,8192]{1,0:T(8,128)(2,1)} %b.1), custom_call_target="tpu_custom_call" | custom-call | tf_op jit(solution)/shard_map/pallas_call | solution.py:337
  1138.1 14.0 %copy.4 = bf16[1024,8192]{1,0:T(8,128)(2,1)} copy(bf16[1024,8192]{1,0:T(8,128)(2,1)} %get-tuple-element.6) | data formatting | bytes 33554432

commit v2 on v1

--- a/solution.py
+++ b/solution.py
@@ -10,6 +10,7 @@
 MESH = pl.DeviceIdType.MESH
 UNITS = 4
 B_BUFFERS = 3
+P_BUFFERS = 4
 
 
 def make_sizes(rows, k_half, cols):
@@ -22,11 +23,12 @@
         unit=rows // UNITS,
         tile=cols // 8,
         x0_depth=k_quarter // 8,
+        tail_depth=max(k_quarter // 32, 128),
         x1_depth=k_quarter // 4,
     )
 
 
-def kernel(sizes, a, b, out, b_far, x0, x1, stage, part, acc, far_s, far_r, x0_s, x0_r, x1_s, x1_r, fwd_s, part_s, part_r, b_sem, x_sem, o_sem):
+def kernel(sizes, a, b, acc, b_far, x0, x1, stage, part, far_s, far_r, x0_s, x0_r, tail_s, tail_r, x1_s, x1_r, fwd_s, part_s, part_r, b_sem, x_sem, o_sem):
     rows, k_half, k_quarter = sizes["rows"], sizes["k_half"], sizes["k_quarter"]
     unit, tile = sizes["unit"], sizes["tile"]
     n_tiles = sizes["cols"] // tile
@@ -56,12 +58,18 @@
     def k_column(kc, depth):
         return pl.multiple_of(lax.rem(r * k_quarter + kc * depth, k_half), depth)
 
-    x0_depth = sizes["x0_depth"]
+    x0_depth, tail_depth = sizes["x0_depth"], sizes["tail_depth"]
     n_x0 = k_half // x0_depth
+    n_tail = x0_depth // tail_depth
 
     def x0_copy(kc):
         block = pl.ds(k_column(kc, x0_depth), x0_depth)
         return remote(a.at[:, block], x0.at[:, block], x0_s.at[kc], x0_r.at[kc], horizontal)
+
+    def tail_copy(kc):
+        block = pl.ds(k_column(kc, tail_depth), tail_depth)
+        q = kc - (n_x0 - 1) * n_tail
+        return remote(a.at[:, block], x0.at[:, block], tail_s.at[q], tail_r.at[q], horizontal)
 
     def unit_rows(u):
         return pl.ds(pl.multiple_of(u * unit, unit), unit)
@@ -86,8 +94,9 @@
 
         lax.fori_loop(0, n, body, 0)
 
-    def own_rows(first, last, source, b_source, ready=None, b_ready=None):
-        base = first if first < n_x0 // 2 else first - n_x0 // 2
+    def own_rows(first, last, source, b_source, ready=None, b_ready=None, depth=x0_depth):
+        far = first * depth >= k_quarter
+        base = first - k_quarter // depth if far else first
         steps = (last - first) * n_tiles
 
         def scope(xbuf, bbuf):
@@ -95,7 +104,7 @@
                 c = lax.div(s, n_tiles)
                 t = lax.rem(s, n_tiles)
                 slot = lax.rem(s, B_BUFFERS)
-                k_rows = pl.ds(pl.multiple_of((base + c) * x0_depth, x0_depth), x0_depth)
+                k_rows = pl.ds(pl.multiple_of((base + c) * depth, depth), depth)
                 return pltpu.make_async_copy(b_source.at[k_rows, tile_cols(t)], bbuf.at[slot], b_sem.at[slot])
 
             def b_start(s):
@@ -122,7 +131,7 @@
                 def _():
                     if ready is not None:
                         ready(first + c)
-                    block = pl.ds(k_column(first + c, x0_depth), x0_depth)
+                    block = pl.ds(k_column(first + c, depth), depth)
                     copy = pltpu.make_async_copy(source.at[:, block], xbuf, x_sem)
                     copy.start()
                     copy.wait()
@@ -146,8 +155,8 @@
 
         pl.run_scoped(
             scope,
-            pltpu.VMEM((rows, x0_depth), jnp.bfloat16),
-            pltpu.VMEM((B_BUFFERS, x0_depth, tile), jnp.bfloat16),
+            pltpu.VMEM((rows, depth), jnp.bfloat16),
+            pltpu.VMEM((B_BUFFERS, depth, tile), jnp.bfloat16),
         )
 
     x1_depth = sizes["x1_depth"]
@@ -217,78 +226,68 @@
             pltpu.VMEM((unit, tile), jnp.float32),
         )
 
-    def finish(units):
-        def scope(pbuf, obuf, p_sem, w_sem):
-            steps = len(units) * n_tiles
-
-            def place(s):
-                u = jnp.int32(units[0])
-                for q in range(1, len(units)):
-                    u = jnp.where(lax.div(s, n_tiles) == q, jnp.int32(units[q]), u)
-                return u, lax.rem(s, n_tiles)
+    def add_parts(first, last):
+        depth = min(P_BUFFERS, last - first)
+
+        def scope(pbuf, p_sem):
+            def fetch(s):
+                where = (unit_rows(lax.div(s, n_tiles)), tile_cols(lax.rem(s, n_tiles)))
+                slot = lax.rem(s, P_BUFFERS)
+                return pltpu.make_async_copy(part.at[where], pbuf.at[slot], p_sem.at[slot])
 
             def start(s):
-                u, t = place(s)
-                slot = lax.rem(s, 2)
-                part_copy(u, t).wait_recv()
-                pltpu.make_async_copy(part.at[unit_rows(u), tile_cols(t)], pbuf.at[slot], p_sem.at[slot]).start()
-
-            def put(s):
-                u, t = place(s)
-                slot = lax.rem(s, 2)
-                return pltpu.make_async_copy(obuf.at[slot], out.at[unit_rows(u), tile_cols(t)], w_sem.at[slot])
-
-            start(jnp.int32(0))
+                part_copy(lax.div(s, n_tiles), lax.rem(s, n_tiles)).wait_recv()
+                fetch(s).start()
+
+            for s in range(first, first + depth - 1):
+                start(jnp.int32(s))
 
             def body(s, carry):
-                u, t = place(s)
-                slot = lax.rem(s, 2)
-
-                @pl.when(s + 1 < steps)
-                def _():
-                    start(s + 1)
-
-                @pl.when(s >= 2)
-                def _():
-                    put(s - 2).wait()
-
-                pltpu.make_async_copy(part.at[unit_rows(u), tile_cols(t)], pbuf.at[slot], p_sem.at[slot]).wait()
-                obuf[slot] = (acc[unit_rows(u), tile_cols(t)] + pbuf[slot]).astype(out.dtype)
-                put(s).start()
+                @pl.when(s + depth - 1 < last)
+                def _():
+                    start(s + depth - 1)
+
+                fetch(s).wait()
+                acc[unit_rows(lax.div(s, n_tiles)), tile_cols(lax.rem(s, n_tiles))] += pbuf[lax.rem(s, P_BUFFERS)]
                 return carry
 
-            lax.fori_loop(0, steps, body, 0)
-            put(jnp.int32(steps - 2)).wait()
-            put(jnp.int32(steps - 1)).wait()
+            lax.fori_loop(first, last, body, 0)
 
         pl.run_scoped(
             scope,
-            pltpu.VMEM((2, unit, tile), jnp.float32),
-            pltpu.VMEM((2, unit, tile), out.dtype),
-            pltpu.SemaphoreType.DMA((2,)),
-            pltpu.SemaphoreType.DMA((2,)),
+            pltpu.VMEM((P_BUFFERS, unit, tile), jnp.float32),
+            pltpu.SemaphoreType.DMA((P_BUFFERS,)),
         )
 
     half = n_x0 // 2
     quarter = n_x0 // 4
+    last = n_x0 - 1
+    tail = (last * n_tail, n_x0 * n_tail)
 
     @pl.when(diag)
     def _():
         each(half, lambda c: x0_copy(c).start())
         each(8, lambda c: far_copy(c).start())
         own_rows(0, half, a, b)
-        own_rows(half, n_x0, a, b_far, b_ready=lambda c: far_copy(c).wait_recv())
-        for u in (0, 1):
-            x1_forward(u).wait_recv()
-            x1_forward(u).start()
-            if u == 1:
-                each(half, lambda c: x0_copy(c + half).start())
+        own_rows(half, n_x0 - 2, a, b_far, b_ready=lambda c: far_copy(c).wait_recv())
+        for c in (6, 7):
+            far_copy(c).wait_recv()
+        x1_forward(0).wait_recv()
+        x1_forward(0).start()
+        other_rows(0)
+        x1_forward(1).wait_recv()
+        x1_forward(1).start()
+        each(half - 1, lambda c: x0_copy(c + half).start())
+        each(n_tail, lambda c: tail_copy(tail[0] + c).start())
+        own_rows(n_x0 - 2, n_x0, a, b_far)
+        for u in (1, 2, 3):
+            if u > 1:
+                x1_forward(u).wait_recv()
             other_rows(u)
-        for u in (2, 3):
-            x1_forward(u).wait_recv()
-            other_rows(u)
-        finish((2, 3, 0, 1))
-        each(n_x0, lambda c: x0_copy(c).wait_send())
+        add_parts(2 * n_tiles, 4 * n_tiles)
+        add_parts(0, 2 * n_tiles)
+        each(last, lambda c: x0_copy(c).wait_send())
+        each(n_tail, lambda c: tail_copy(tail[0] + c).wait_send())
         for u in (0, 1):
             x1_forward(u).wait_send()
 
@@ -312,8 +311,14 @@
         for u in (0, 1):
             x1_forward(u).wait_recv()
             other_rows(u)
-        own_rows(half, n_x0, x0, b_far, ready=arrived)
-        finish((0, 1, 2, 3))
+        own_rows(half, half + 4, x0, b_far, ready=arrived)
+        add_parts(0, 2 * n_tiles)
+        own_rows(half + 4, last - 1, x0, b_far, ready=arrived)
+        add_parts(2 * n_tiles, 3 * n_tiles)
+        own_rows(last - 1, last, x0, b_far, ready=arrived)
+        add_parts(3 * n_tiles, 3 * n_tiles + 6)
+        own_rows(*tail, x0, b_far, ready=lambda c: tail_copy(c).wait_recv(), depth=tail_depth)
+        add_parts(3 * n_tiles + 6, 4 * n_tiles)
         for u in range(UNITS):
             x1_send(u, vertical).wait_send()
         for u in (2, 3):
@@ -332,12 +337,13 @@
         k_quarter, cols = b_block.shape
         sizes = make_sizes(rows, k_half, cols)
         n_x0 = k_half // sizes["x0_depth"]
+        n_tail = sizes["x0_depth"] // sizes["tail_depth"]
         n_part = UNITS * (cols // sizes["tile"])
         dma = pltpu.SemaphoreType.DMA
         results = pl.pallas_call(
             functools.partial(kernel, sizes),
             out_shape=[
-                jax.ShapeDtypeStruct((rows, cols), jnp.bfloat16),
+                pltpu.VMEM((rows, cols), jnp.float32),
                 jax.ShapeDtypeStruct((k_quarter, cols), jnp.bfloat16),
                 jax.ShapeDtypeStruct((rows, k_half), jnp.bfloat16),
                 jax.ShapeDtypeStruct((rows, k_half), jnp.bfloat16),
@@ -345,13 +351,14 @@
                 jax.ShapeDtypeStruct((rows, cols), jnp.float32),
             ],
             in_specs=[pl.BlockSpec(memory_space=pl.ANY)] * 2,
-            out_specs=[pl.BlockSpec(memory_space=pl.ANY)] * 6,
+            out_specs=[pl.BlockSpec(memory_space=pltpu.VMEM)] + [pl.BlockSpec(memory_space=pl.ANY)] * 5,
             scratch_shapes=[
-                pltpu.VMEM((rows, cols), jnp.float32),
                 dma((8,)),
                 dma((8,)),
                 dma((n_x0,)),
                 dma((n_x0,)),
+                dma((n_tail,)),
+                dma((n_tail,)),
                 dma((UNITS,)),
                 dma((UNITS,)),
                 dma((UNITS,)),
@@ -362,9 +369,9 @@
                 dma,
             ],
             compiler_params=pltpu.CompilerParams(
-                collective_id=0, has_side_effects=True, vmem_limit_bytes=63 * 1024 * 1024
+                collective_id=0, has_side_effects=True, vmem_limit_bytes=30 * 1024 * 1024
             ),
         )(a_block, b_block)
-        return results[0]
+        return results[0].astype(jnp.bfloat16)
 
     return jax.shard_map(local_block, mesh=mesh, in_specs=(grid_spec, grid_spec), out_specs=grid_spec, check_vma=False)

time: 1150 us -> 1100 us (0.957)
  Pallas kernels: 1140 us -> 1090 us
  local copies, waits for them, and re-layouts: 14 us -> 0 us
    pallas_call x1, Pallas kernels: 1140 us -> 1090 us  [local_block(): pl.pallas_call(functools.partial(kernel, sizes), out_shape=[pltpu.VMEM((r...]
    unnamed x1 -> x0, local copies, waits for them, and re-layouts: 14 us -> none
where the time goes in v2:
time: 1100 us
  Pallas kernels  1090 us (99%)
    pallas_call x1, Pallas kernels, local_block(): pl.pallas_call(functools.partial(kernel, sizes), out_shape=[pltpu.VMEM((r...  1090 us

profile of v2, /device:TPU:2, one launch (start us, length us, event | category | flops | bytes accessed | tf_op | source)
XLA Modules:
  0.0 1101.0 jit_solution(12334003387854800322)
XLA Ops:
  0.0 1094.0 %shard_map.28 = (f32[1024,8192]{1,0:T(8,128)S(1)}, bf16[8192,8192]{1,0:T(8,128)(2,1)}, bf16[1024,16384]{1,0:T(8,128)(2,1)}, bf16[1024,16384]{1,0:T(8,128)(2,1)},...) custom-call(bf16[1024,16384]{1,0:T(8,128)(2,1)} %a.1, bf16[8192,8192]{1,0:T(8,128)(2,1)} %b.1), custom_call_target="tpu_custom_call" | custom-call | tf_op jit(solution)/shard_map/pallas_call | solution.py:343
  1094.0 7.0 convert_element_type.3

commit v3 on v2

--- a/solution.py
+++ b/solution.py
@@ -23,12 +23,12 @@
         unit=rows // UNITS,
         tile=cols // 8,
         x0_depth=k_quarter // 8,
-        tail_depth=max(k_quarter // 32, 128),
+        tail_depth=k_quarter // 16,
         x1_depth=k_quarter // 4,
     )
 
 
-def kernel(sizes, a, b, acc, b_far, x0, x1, stage, part, far_s, far_r, x0_s, x0_r, tail_s, tail_r, x1_s, x1_r, fwd_s, part_s, part_r, b_sem, x_sem, o_sem):
+def kernel(sizes, a, b, acc, b_far, x0, x1, stage, part, far_s, far_r, x_last, part_last, x0_s, x0_r, tail_s, tail_r, last_s, last_r, x1_s, x1_r, fwd_s, part_s, part_r, end_s, end_r, b_sem, x_sem, o_sem):
     rows, k_half, k_quarter = sizes["rows"], sizes["k_half"], sizes["k_quarter"]
     unit, tile = sizes["unit"], sizes["tile"]
     n_tiles = sizes["cols"] // tile
@@ -58,9 +58,12 @@
     def k_column(kc, depth):
         return pl.multiple_of(lax.rem(r * k_quarter + kc * depth, k_half), depth)
 
+    def unit_rows(u):
+        return pl.ds(pl.multiple_of(u * unit, unit), unit)
+
     x0_depth, tail_depth = sizes["x0_depth"], sizes["tail_depth"]
     n_x0 = k_half // x0_depth
-    n_tail = x0_depth // tail_depth
+    n_tail = k_half // tail_depth
 
     def x0_copy(kc):
         block = pl.ds(k_column(kc, x0_depth), x0_depth)
@@ -68,11 +71,12 @@
 
     def tail_copy(kc):
         block = pl.ds(k_column(kc, tail_depth), tail_depth)
-        q = kc - (n_x0 - 1) * n_tail
+        q = kc - n_tail // 2
         return remote(a.at[:, block], x0.at[:, block], tail_s.at[q], tail_r.at[q], horizontal)
 
-    def unit_rows(u):
-        return pl.ds(pl.multiple_of(u * unit, unit), unit)
+    def last_copy(q):
+        block = pl.ds(k_column(n_tail - 1, tail_depth), tail_depth)
+        return remote(a.at[unit_rows(q), block], x_last.at[unit_rows(q)], last_s.at[q], last_r.at[q], horizontal)
 
     def x1_send(u, device):
         return remote(a.at[unit_rows(u)], x1.at[unit_rows(u)], x1_s.at[u], x1_r.at[u], device)
@@ -86,6 +90,9 @@
     def part_copy(u, t):
         where = (unit_rows(u), tile_cols(t))
         return remote(stage.at[where], part.at[where], part_s.at[u * n_tiles + t], part_r.at[u * n_tiles + t], vertical)
+
+    def end_copy(u):
+        return remote(stage.at[unit_rows(u), tile_cols(n_tiles - 1)], part_last, end_s, end_r, vertical)
 
     def each(n, step):
         def body(c, carry):
@@ -162,7 +169,7 @@
     x1_depth = sizes["x1_depth"]
     n_x1 = k_half // x1_depth
 
-    def other_rows(u):
+    def other_rows(u, final=False):
         steps = n_tiles * n_x1
 
         def scope(xbuf, bbuf, pbuf):
@@ -213,7 +220,17 @@
                     put = pltpu.make_async_copy(pbuf, stage.at[unit_rows(u), tile_cols(t)], o_sem)
                     put.start()
                     put.wait()
-                    part_copy(u, t).start()
+                    if final:
+
+                        @pl.when(t < n_tiles - 1)
+                        def _():
+                            part_copy(u, t).start()
+
+                        @pl.when(t == n_tiles - 1)
+                        def _():
+                            end_copy(u).start()
+                    else:
+                        part_copy(u, t).start()
 
                 return carry
 
@@ -226,8 +243,8 @@
             pltpu.VMEM((unit, tile), jnp.float32),
         )
 
-    def add_parts(first, last):
-        depth = min(P_BUFFERS, last - first)
+    def add_parts(first, last, depth=P_BUFFERS):
+        depth = min(depth, last - first)
 
         def scope(pbuf, p_sem):
             def fetch(s):
@@ -259,10 +276,34 @@
             pltpu.SemaphoreType.DMA((P_BUFFERS,)),
         )
 
+    def add_end(u):
+        end_copy(u).wait_recv()
+        acc[unit_rows(u), tile_cols(n_tiles - 1)] += part_last[...]
+
+    def last_rows(before, between):
+        def scope(bbuf):
+            load = pltpu.make_async_copy(b_far.at[pl.ds(k_quarter - tail_depth, tail_depth)], bbuf, o_sem)
+            load.start()
+            before()
+            load.wait()
+
+            def step(q):
+                last_copy(q).wait_recv()
+                for t in range(n_tiles):
+                    columns = pl.ds(t * tile, tile)
+                    acc[unit_rows(q), columns] += jnp.dot(
+                        x_last[unit_rows(q), :], bbuf[:, columns], preferred_element_type=jnp.float32
+                    )
+
+            each(UNITS - 1, step)
+            between()
+            each(1, lambda q: step(q + UNITS - 1))
+
+        pl.run_scoped(scope, pltpu.VMEM((tail_depth, sizes["cols"]), jnp.bfloat16))
+
     half = n_x0 // 2
     quarter = n_x0 // 4
-    last = n_x0 - 1
-    tail = (last * n_tail, n_x0 * n_tail)
+    thin = n_tail // 2
 
     @pl.when(diag)
     def _():
@@ -277,19 +318,26 @@
         other_rows(0)
         x1_forward(1).wait_recv()
         x1_forward(1).start()
-        each(half - 1, lambda c: x0_copy(c + half).start())
-        each(n_tail, lambda c: tail_copy(tail[0] + c).start())
+        each(thin - 1, lambda c: tail_copy(thin + c).start())
+        each(UNITS, lambda q: last_copy(q).start())
         own_rows(n_x0 - 2, n_x0, a, b_far)
-        for u in (1, 2, 3):
-            if u > 1:
-                x1_forward(u).wait_recv()
-            other_rows(u)
+        other_rows(1)
+        for u in (2, 3):
+            x1_forward(u).wait_recv()
+            other_rows(u, final=u == 3)
         add_parts(2 * n_tiles, 4 * n_tiles)
-        add_parts(0, 2 * n_tiles)
-        each(last, lambda c: x0_copy(c).wait_send())
-        each(n_tail, lambda c: tail_copy(tail[0] + c).wait_send())
+        add_parts(0, n_tiles)
+        add_parts(n_tiles, 2 * n_tiles - 1, depth=1)
+        add_end(1)
+        each(half, lambda c: x0_copy(c).wait_send())
+        each(thin - 1, lambda c: tail_copy(thin + c).wait_send())
+        each(UNITS, lambda q: last_copy(q).wait_send())
         for u in (0, 1):
             x1_forward(u).wait_send()
+        for u in (0, 1, 2):
+            each(n_tiles, lambda t: part_copy(u, t).wait_send())
+        each(n_tiles - 1, lambda t: part_copy(3, t).wait_send())
+        end_copy(3).wait_send()
 
     @pl.when(off)
     def _():
@@ -310,23 +358,30 @@
         other_rows(3)
         for u in (0, 1):
             x1_forward(u).wait_recv()
-            other_rows(u)
-        own_rows(half, half + 4, x0, b_far, ready=arrived)
+            other_rows(u, final=u == 1)
+        thin_arrived = lambda c: tail_copy(c).wait_recv()
+        rest = lambda first, last: own_rows(first, last, x0, b_far, ready=thin_arrived, depth=tail_depth)
+        rest(thin, thin + 8)
         add_parts(0, 2 * n_tiles)
-        own_rows(half + 4, last - 1, x0, b_far, ready=arrived)
-        add_parts(2 * n_tiles, 3 * n_tiles)
-        own_rows(last - 1, last, x0, b_far, ready=arrived)
-        add_parts(3 * n_tiles, 3 * n_tiles + 6)
-        own_rows(*tail, x0, b_far, ready=lambda c: tail_copy(c).wait_recv(), depth=tail_depth)
-        add_parts(3 * n_tiles + 6, 4 * n_tiles)
+        rest(thin + 8, n_tail - 4)
+        add_parts(2 * n_tiles, 3 * n_tiles + 4)
+        rest(n_tail - 4, n_tail - 2)
+        add_parts(3 * n_tiles + 4, 3 * n_tiles + 6)
+        last_rows(
+            before=lambda: rest(n_tail - 2, n_tail - 1),
+            between=lambda: add_parts(3 * n_tiles + 6, 4 * n_tiles - 1),
+        )
+        add_end(3)
         for u in range(UNITS):
             x1_send(u, vertical).wait_send()
         for u in (2, 3):
             x1_forward(u).wait_send()
+        for u in (0, 2, 3):
+            each(n_tiles, lambda t: part_copy(u, t).wait_send())
+        each(n_tiles - 1, lambda t: part_copy(1, t).wait_send())
+        end_copy(1).wait_send()
 
     each(8, lambda c: far_copy(c).wait_send())
-    for u in range(UNITS):
-        each(n_tiles, lambda t: part_copy(u, t).wait_send())
 
 
 def solution(mesh):
@@ -337,7 +392,7 @@
         k_quarter, cols = b_block.shape
         sizes = make_sizes(rows, k_half, cols)
         n_x0 = k_half // sizes["x0_depth"]
-        n_tail = sizes["x0_depth"] // sizes["tail_depth"]
+        n_tail = k_half // sizes["tail_depth"]
         n_part = UNITS * (cols // sizes["tile"])
         dma = pltpu.SemaphoreType.DMA
         results = pl.pallas_call(
@@ -355,15 +410,21 @@
             scratch_shapes=[
                 dma((8,)),
                 dma((8,)),
-                dma((n_x0,)),
-                dma((n_x0,)),
-                dma((n_tail,)),
-                dma((n_tail,)),
+                pltpu.VMEM((rows, sizes["tail_depth"]), jnp.bfloat16),
+                pltpu.VMEM((sizes["unit"], sizes["tile"]), jnp.float32),
+                dma((n_x0 // 2,)),
+                dma((n_x0 // 2,)),
+                dma((n_tail // 2 - 1,)),
+                dma((n_tail // 2 - 1,)),
+                dma((UNITS,)),
+                dma((UNITS,)),
                 dma((UNITS,)),
                 dma((UNITS,)),
                 dma((UNITS,)),
                 dma((n_part,)),
                 dma((n_part,)),
+                dma,
+                dma,
                 dma((B_BUFFERS,)),
                 dma,
                 dma,

time: 1100 us -> 1090 us (level)
  no operation moved by 1% of the time
where the time goes in v3:
time: 1090 us
  Pallas kernels  1090 us (100%)
    pallas_call x1, Pallas kernels, local_block(): pl.pallas_call(functools.partial(kernel, sizes), out_shape=[pltpu.VMEM((r...  1090 us

profile of v3, /device:TPU:2, one launch (start us, length us, event | category | flops | bytes accessed | tf_op | source)
XLA Modules:
  0.0 1093.3 jit_solution(5588691136367358716)
XLA Ops:
  0.0 1086.3 %shard_map.28 = (f32[1024,8192]{1,0:T(8,128)S(1)}, bf16[8192,8192]{1,0:T(8,128)(2,1)}, bf16[1024,16384]{1,0:T(8,128)(2,1)}, bf16[1024,16384]{1,0:T(8,128)(2,1)},...) custom-call(bf16[1024,16384]{1,0:T(8,128)(2,1)} %a.1, bf16[8192,8192]{1,0:T(8,128)(2,1)} %b.1), custom_call_target="tpu_custom_call" | custom-call | tf_op jit(solution)/shard_map/pallas_call | solution.py:398
  1086.3 7.0 convert_element_type.3

commit v4 on v3

--- a/solution.py
+++ b/solution.py
@@ -11,6 +11,8 @@
 UNITS = 4
 B_BUFFERS = 3
 P_BUFFERS = 4
+R_BUFFERS = 8
+R_ROWS = 32
 
 
 def make_sizes(rows, k_half, cols):
@@ -382,6 +384,46 @@
         end_copy(1).wait_send()
 
     each(8, lambda c: far_copy(c).wait_send())
+
+
+def round_kernel(steps, acc, out, buf, sem):
+    height = acc.shape[0] // steps
+
+    def rows_of(s):
+        return pl.ds(pl.multiple_of(s * height, height), height)
+
+    def put(s):
+        slot = lax.rem(s, R_BUFFERS)
+        return pltpu.make_async_copy(buf.at[slot], out.at[rows_of(s)], sem.at[slot])
+
+    def body(s, carry):
+        @pl.when(s >= R_BUFFERS)
+        def _():
+            put(s - R_BUFFERS).wait()
+
+        buf[lax.rem(s, R_BUFFERS)] = acc[rows_of(s), :].astype(out.dtype)
+        put(s).start()
+        return carry
+
+    lax.fori_loop(0, steps, body, 0)
+    for s in range(steps - R_BUFFERS, steps):
+        put(jnp.int32(s)).wait()
+
+
+def rounded(acc):
+    rows, cols = acc.shape
+    steps = max(rows // R_ROWS, R_BUFFERS)
+    return pl.pallas_call(
+        functools.partial(round_kernel, steps),
+        out_shape=jax.ShapeDtypeStruct((rows, cols), jnp.bfloat16),
+        in_specs=[pl.BlockSpec(memory_space=pltpu.VMEM)],
+        out_specs=pl.BlockSpec(memory_space=pl.ANY),
+        scratch_shapes=[
+            pltpu.VMEM((R_BUFFERS, rows // steps, cols), jnp.bfloat16),
+            pltpu.SemaphoreType.DMA((R_BUFFERS,)),
+        ],
+        compiler_params=pltpu.CompilerParams(vmem_limit_bytes=20 * 1024 * 1024),
+    )(pltpu.with_memory_space_constraint(acc, pltpu.VMEM))
 
 
 def solution(mesh):
@@ -433,6 +475,6 @@
                 collective_id=0, has_side_effects=True, vmem_limit_bytes=30 * 1024 * 1024
             ),
         )(a_block, b_block)
-        return results[0].astype(jnp.bfloat16)
+        return rounded(results[0])
 
     return jax.shard_map(local_block, mesh=mesh, in_specs=(grid_spec, grid_spec), out_specs=grid_spec, check_vma=False)

time: 1090 us -> 1090 us (level)
  no operation moved by 1% of the time
where the time goes in v4:
time: 1090 us
  Pallas kernels  1090 us (100%)
    pallas_call x1, Pallas kernels, local_block(): pl.pallas_call(functools.partial(kernel, sizes), out_shape=[pltpu.VMEM((r...  1090 us

profile of v4, /device:TPU:2, one launch (start us, length us, event | category | flops | bytes accessed | tf_op | source)
XLA Modules:
  0.0 1092.4 jit_solution(10209686385236027183)
XLA Ops:
  0.0 1086.3 %shard_map.28 = (f32[1024,8192]{1,0:T(8,128)S(1)}, bf16[8192,8192]{1,0:T(8,128)(2,1)}, bf16[1024,16384]{1,0:T(8,128)(2,1)}, bf16[1024,16384]{1,0:T(8,128)(2,1)},...) custom-call(bf16[1024,16384]{1,0:T(8,128)(2,1)} %a.1, bf16[8192,8192]{1,0:T(8,128)(2,1)} %b.1), custom_call_target="tpu_custom_call" | custom-call | tf_op jit(solution)/shard_map/pallas_call | solution.py:440
  1086.3 5.9 shard_map.29

commit v5 on v4

--- a/solution.py
+++ b/solution.py
@@ -11,6 +11,7 @@
 UNITS = 4
 B_BUFFERS = 3
 P_BUFFERS = 4
+PIECES = 8
 R_BUFFERS = 8
 R_ROWS = 32
 
@@ -76,9 +77,12 @@
         q = kc - n_tail // 2
         return remote(a.at[:, block], x0.at[:, block], tail_s.at[q], tail_r.at[q], horizontal)
 
+    def piece_rows(q):
+        return pl.ds(pl.multiple_of(q * (rows // PIECES), rows // PIECES), rows // PIECES)
+
     def last_copy(q):
         block = pl.ds(k_column(n_tail - 1, tail_depth), tail_depth)
-        return remote(a.at[unit_rows(q), block], x_last.at[unit_rows(q)], last_s.at[q], last_r.at[q], horizontal)
+        return remote(a.at[piece_rows(q), block], x_last.at[piece_rows(q)], last_s.at[q], last_r.at[q], horizontal)
 
     def x1_send(u, device):
         return remote(a.at[unit_rows(u)], x1.at[unit_rows(u)], x1_s.at[u], x1_r.at[u], device)
@@ -293,13 +297,13 @@
                 last_copy(q).wait_recv()
                 for t in range(n_tiles):
                     columns = pl.ds(t * tile, tile)
-                    acc[unit_rows(q), columns] += jnp.dot(
-                        x_last[unit_rows(q), :], bbuf[:, columns], preferred_element_type=jnp.float32
+                    acc[piece_rows(q), columns] += jnp.dot(
+                        x_last[piece_rows(q), :], bbuf[:, columns], preferred_element_type=jnp.float32
                     )
 
-            each(UNITS - 1, step)
+            each(PIECES - 1, step)
             between()
-            each(1, lambda q: step(q + UNITS - 1))
+            each(1, lambda q: step(q + PIECES - 1))
 
         pl.run_scoped(scope, pltpu.VMEM((tail_depth, sizes["cols"]), jnp.bfloat16))
 
@@ -321,7 +325,7 @@
         x1_forward(1).wait_recv()
         x1_forward(1).start()
         each(thin - 1, lambda c: tail_copy(thin + c).start())
-        each(UNITS, lambda q: last_copy(q).start())
+        each(PIECES, lambda q: last_copy(q).start())
         own_rows(n_x0 - 2, n_x0, a, b_far)
         other_rows(1)
         for u in (2, 3):
@@ -333,7 +337,7 @@
         add_end(1)
         each(half, lambda c: x0_copy(c).wait_send())
         each(thin - 1, lambda c: tail_copy(thin + c).wait_send())
-        each(UNITS, lambda q: last_copy(q).wait_send())
+        each(PIECES, lambda q: last_copy(q).wait_send())
         for u in (0, 1):
             x1_forward(u).wait_send()
         for u in (0, 1, 2):
@@ -458,8 +462,8 @@
                 dma((n_x0 // 2,)),
                 dma((n_tail // 2 - 1,)),
                 dma((n_tail // 2 - 1,)),
-                dma((UNITS,)),
-                dma((UNITS,)),
+                dma((PIECES,)),
+                dma((PIECES,)),
                 dma((UNITS,)),
                 dma((UNITS,)),
                 dma((UNITS,)),

time: 1090 us -> 1090 us (level)
  no operation moved by 1% of the time
where the time goes in v5:
time: 1090 us
  Pallas kernels  1090 us (100%)
    pallas_call x1, Pallas kernels, local_block(): pl.pallas_call(functools.partial(kernel, sizes), out_shape=[pltpu.VMEM((r...  1090 us

profile of v5, /device:TPU:2, one launch (start us, length us, event | category | flops | bytes accessed | tf_op | source)
XLA Modules:
  0.0 1092.3 jit_solution(4748747465133819769)
XLA Ops:
  0.0 1086.2 %shard_map.28 = (f32[1024,8192]{1,0:T(8,128)S(1)}, bf16[8192,8192]{1,0:T(8,128)(2,1)}, bf16[1024,16384]{1,0:T(8,128)(2,1)}, bf16[1024,16384]{1,0:T(8,128)(2,1)},...) custom-call(bf16[1024,16384]{1,0:T(8,128)(2,1)} %a.1, bf16[8192,8192]{1,0:T(8,128)(2,1)} %b.1), custom_call_target="tpu_custom_call" | custom-call | tf_op jit(solution)/shard_map/pallas_call | solution.py:444
  1086.2 5.9 shard_map.29
